TPU v7x, 32 devices: a whole 2x2x4 slice. The times are simulated.
32 devices in a mesh: groups: 2 (over y), slab: 4 (over z), pencil: 2 (over x), comp: 2 (over core).
Axes of the slice: x: 2, y: 2, z: 4, core: 2. Of those that a mesh axis runs over, the one named last changes fastest.
Arguments:
- u_start: float32 [3, 64, 64, 512], P(None, ('groups', 'slab'), 'pencil', 'comp'), parts along dimension 1, may hold values from -6 to 6
- toughness: float32 [64, 64, 512], P(('groups', 'slab'), 'pencil', 'comp'), parts along dimension 0, may hold values from 0.3 to 1.5
- crack_label: int32 [64, 64, 512], P(('groups', 'slab'), 'pencil', 'comp'), parts along dimension 0, may hold values from 0 to 2
- obs_weight: bfloat16 [32, 64, 2, 4096], P('slab', 'pencil', 'comp'), may hold values from -0.75 to 0.75
- sensor_cell: int32 [4096], replicated, may hold values from 0 to 4095
Outputs:
- moved: float32 [3, 64, 64, 512], P(None, ('groups', 'slab'), 'pencil', 'comp'), parts along dimension 1
- damage: float32 [64, 64, 512], P(('groups', 'slab'), 'pencil', 'comp'), parts along dimension 0
- readings: float32 [3, 8192], P(None, 'groups'), parts along dimension 1
There are 2 independent parts, one for each index of `groups`. A program takes and returns all parts, laid end to end along the dimension named above; an argument that names none is the same for every part. Nothing has to cross between parts.
Inputs may be any that keep to these rules, and one draw needn't show every extreme that they name: `sensor_cell`: numbers cell blocks as (64 z + y) * 2 + h. `crack_label`: 0 intact, 1 partly cracked, 2 cracked.
All inputs are finite; a program needn't handle non-finite values.
Results may differ from a plain program's by a relative error of at most 0.003.
Values sent between devices are 32-bit elements; how exact they have to be, the bound alone decides.
A program may use at most 128 MiB of HBM per device.

v0:
```python
import jax
import jax.numpy as jnp
from jax import lax
from jax.sharding import PartitionSpec as P

SHEAR_MODULUS = 1.0
LAME_FIRST = 1.5
RESIDUAL_STIFF = 0.001
TIME_DISP = 0.15
TIME_DAMAGE = 0.08
LENGTH_SCALE = 1.0
DAMAGE_LEVEL = 0.45
POINT_GAIN = 8.0


def with_halo(block, sides, width):
    for axis, dim in sides:
        count = lax.axis_size(axis)
        forward = [(i, i + 1) for i in range(count - 1)]
        backward = [(target, source) for source, target in forward]
        low = lax.ppermute(
            lax.slice_in_dim(block, block.shape[dim] - width, None, axis=dim), axis, forward
        )
        high = lax.ppermute(lax.slice_in_dim(block, 0, width, axis=dim), axis, backward)
        block = jnp.concatenate([low, block, high], axis=dim)
    return block


def central(source, spatial):
    if spatial == 0:
        return 0.5 * (source[..., 2:, 1:-1, 1:-1] - source[..., :-2, 1:-1, 1:-1])
    if spatial == 1:
        return 0.5 * (source[..., 1:-1, 2:, 1:-1] - source[..., 1:-1, :-2, 1:-1])
    return 0.5 * (source[..., 1:-1, 1:-1, 2:] - source[..., 1:-1, 1:-1, :-2])


def shrink(source):
    return source[..., 1:-1, 1:-1, 1:-1]


def laplace(source):
    return (
        source[2:, 1:-1, 1:-1]
        + source[:-2, 1:-1, 1:-1]
        + source[1:-1, 2:, 1:-1]
        + source[1:-1, :-2, 1:-1]
        + source[1:-1, 1:-1, 2:]
        + source[1:-1, 1:-1, :-2]
        - 6.0 * source[1:-1, 1:-1, 1:-1]
    )


def entry_key(first, second):
    return (min(first, second), max(first, second))


def rotate(matrix, first, second):
    other = 3 - first - second
    diag_first = matrix[first, first]
    diag_second = matrix[second, second]
    coupling = matrix[first, second]
    angle = 0.5 * jnp.arctan2(2.0 * coupling, diag_second - diag_first)
    cosine = jnp.cos(angle)
    sine = jnp.sin(angle)
    side_first = matrix[entry_key(other, first)]
    side_second = matrix[entry_key(other, second)]
    result = dict(matrix)
    result[first, first] = (
        cosine * cosine * diag_first - 2.0 * cosine * sine * coupling + sine * sine * diag_second
    )
    result[second, second] = (
        sine * sine * diag_first + 2.0 * cosine * sine * coupling + cosine * cosine * diag_second
    )
    result[first, second] = jnp.zeros_like(coupling)
    result[entry_key(other, first)] = cosine * side_first - sine * side_second
    result[entry_key(other, second)] = sine * side_first + cosine * side_second
    return result


def eigenvalues(matrix):
    for sweep_index in range(5):
        for first, second in ((0, 1), (0, 2), (1, 2)):
            matrix = rotate(matrix, first, second)
    return [matrix[0, 0], matrix[1, 1], matrix[2, 2]]


def advance(padded_disp, padded_damage, toughness):
    gradient = [
        [central(padded_disp[component], direction) for direction in range(3)]
        for component in range(3)
    ]
    strain = {}
    for first in range(3):
        for second in range(first, 3):
            strain[first, second] = 0.5 * (gradient[first][second] + gradient[second][first])
    trace_full = strain[0, 0] + strain[1, 1] + strain[2, 2]
    damage_mid = shrink(padded_damage)
    degrade = (1.0 - damage_mid) ** 2 + RESIDUAL_STIFF
    divergence = []
    for component in range(3):
        total_force = 0.0
        for direction in range(3):
            stress = 2.0 * SHEAR_MODULUS * strain[entry_key(component, direction)]
            if component == direction:
                stress = stress + LAME_FIRST * trace_full
            total_force = total_force + central(degrade * stress, direction)
        divergence.append(total_force)
    moved = shrink(shrink(padded_disp)) + TIME_DISP * jnp.stack(divergence)
    inner = {key_pair: shrink(entry_value) for key_pair, entry_value in strain.items()}
    trace_inner = shrink(trace_full)
    energy = 0.5 * LAME_FIRST * jnp.maximum(trace_inner, 0.0) ** 2
    for eigen_value in eigenvalues(inner):
        energy = energy + SHEAR_MODULUS * jnp.maximum(eigen_value, 0.0) ** 2
    damage_core = shrink(damage_mid)
    damage = damage_core + TIME_DAMAGE * (
        2.0 * (1.0 - damage_core) * energy
        - toughness / LENGTH_SCALE * damage_core
        + toughness * LENGTH_SCALE * laplace(damage_mid)
    )
    return (moved, damage)


def local(u_start, toughness, crack_label, obs_weight, sensor_cell):
    planes, rows, columns = toughness.shape
    damage = DAMAGE_LEVEL * crack_label.astype(jnp.float32)
    moved = u_start
    for repeat in range(2):
        stacked = jnp.concatenate([moved, damage[None]], axis=0)
        padded = with_halo(stacked, (("slab", 1), ("pencil", 2), ("comp", 3)), 2)
        moved, damage = advance(padded[:3], padded[3], toughness)
    pooled = jnp.mean(moved, axis=-1).reshape(3, planes * rows).astype(jnp.bfloat16)
    weight_rows = obs_weight.reshape(planes * rows, obs_weight.shape[-1])
    dense = jnp.dot(pooled, weight_rows, preferred_element_type=jnp.float32)
    plane_ids = lax.axis_index("slab") * planes + jnp.arange(planes, dtype=jnp.int32)
    row_ids = lax.axis_index("pencil") * rows + jnp.arange(rows, dtype=jnp.int32)
    block_ids = (
        (plane_ids[:, None] * (rows * lax.axis_size("pencil")) + row_ids[None, :])
        * lax.axis_size("comp")
        + lax.axis_index("comp")
    ).reshape(planes * rows)
    picks = (block_ids[:, None] == sensor_cell[None, :]).astype(jnp.bfloat16)
    point = jnp.dot(pooled, picks, preferred_element_type=jnp.float32)
    partial_sum = dense + POINT_GAIN * point
    readings = lax.psum(partial_sum, ("slab", "pencil", "comp"))
    return (moved, damage, readings)


def solution(mesh):
    return jax.shard_map(
        local,
        mesh=mesh,
        in_specs=(
            P(None, ("groups", "slab"), "pencil", "comp"),
            P(("groups", "slab"), "pencil", "comp"),
            P(("groups", "slab"), "pencil", "comp"),
            P("slab", "pencil", "comp", None),
            P(),
        ),
        out_specs=(
            P(None, ("groups", "slab"), "pencil", "comp"),
            P(("groups", "slab"), "pencil", "comp"),
            P(None, "groups"),
        ),
        check_vma=False,
    )
```

profile of v0, /device:TPU:0, one launch (start us, length us, event | category | flops | bytes accessed | tf_op | source)
XLA Modules:
  0.0 226.6 jit_solution(18250146474018214217)
XLA Ops:
  2.9 5.0 %collective-permute-start = (f32[4,2,32,256]{3,2,1,0:T(8,128)S(1)}, f32[4,2,32,256]{3,2,1,0:T(8,128)S(1)}, u32[]{:S(2)}, u32[]{:S(2)}) collective-permute-start(f32[4,2,32,256]{3,2,1,0:T(8,128)S(1)} %get-tuple-element.66), channel_id=1, source_target_pairs={{0,4},{4,8},{8,12},{1,5},{5,9},{9,13},{2,6},{6,10},{10,14},{3,7},{... | collective-permute-start | bytes 786440 | tf_op jit(solution)/shard_map/ppermute | solution.py:21
  9.1 4.2 %collective-permute-done = f32[4,2,32,256]{3,2,1,0:T(8,128)S(1)} collective-permute-done((f32[4,2,32,256]{3,2,1,0:T(8,128)S(1)}, f32[4,2,32,256]{3,2,1,0:T(8,128)S(1)}, u32[]{:S(2)}, u32[]{:S(2)}) %collective-permute-start) | collective-permute-done | bytes 262176 | tf_op jit(solution)/shard_map/ppermute | solution.py:21
  13.4 4.1 %collective-permute-done.1 = f32[4,2,32,256]{3,2,1,0:T(8,128)S(1)} collective-permute-done((f32[4,2,32,256]{3,2,1,0:T(8,128)S(1)}, f32[4,2,32,256]{3,2,1,0:T(8,128)S(1)}, u32[]{:S(2)}, u32[]{:S(2)}) %collective-permute-start.1) | collective-permute-done | bytes 262176 | tf_op jit(solution)/shard_map/ppermute | solution.py:24
  18.7 3.4 %collective-permute-start.2 = (f32[4,12,2,256]{3,2,1,0:T(2,128)S(1)}, f32[4,12,2,256]{3,2,1,0:T(2,128)S(1)}, u32[]{:S(2)}, u32[]{:S(2)}) collective-permute-start(f32[4,12,2,256]{3,2,1,0:T(2,128)S(1)} %get-tuple-element.58), channel_id=1, source_target_pairs={{0,2},{1,3},{4,6},{5,7},{8,10},{9,11},{12,14},{13,15},{16,18},{17,... | collective-permute-start | bytes 294920 | tf_op jit(solution)/shard_map/ppermute | solution.py:21
  24.3 4.3 %collective-permute-done.3 = f32[4,12,2,256]{3,2,1,0:T(2,128)S(1)} collective-permute-done((f32[4,12,2,256]{3,2,1,0:T(2,128)S(1)}, f32[4,12,2,256]{3,2,1,0:T(2,128)S(1)}, u32[]{:S(2)}, u32[]{:S(2)}) %collective-permute-start.3) | collective-permute-done | bytes 98336 | tf_op jit(solution)/shard_map/ppermute | solution.py:24
  34.1 2.2 copy.25
  37.6 2.2 copy.26
  39.8 2.2 copy.27
  42.0 3.1 %pad_maximum_fusion = f32[4,12,36,260]{3,2,1,0:T(8,128)S(1)} fusion(f32[4,12,36,2]{3,2,1,0:T(8,128)} %copy.27, f32[4,12,2,256]{3,2,1,0:T(2,128)} %copy-done.13, f32[4,2,32,256]{3,2,1,0:T(8,128)} %copy-done.5, f32[1,8,32,256]{3,2,1,0:T(8,128)S(1)} %multiply_bitcast_fusion, f32[3,8,32,256]{3,2,1,0:T(8,128)S(1)} %copy-done.1, ...), kind=kLoop, calls=%fused_computation.3 | loop fusion | flops 3144960 | bytes 3594240 | tf_op jit(solution)/shard_map/concatenate | solution.py:25
  45.3 2.2 multiply_multiply_fusion.5
  50.1 29.3 %fusion.51 = f32[1,8,32,256]{3,2,1,0:T(8,128)S(1)} fusion(f32[8,32,256]{2,1,0:T(8,128)S(1)} %copy-done.15, f32[12,36,260]{2,1,0:T(8,128)S(1)} %get-tuple-element.37, f32[10,34,258]{2,1,0:T(8,128)S(1)} %get-tuple-element.46, f32[10,34,258]{2,1,0:T(8,128)S(1)} %get-tuple-element.47, f32[10,34,258]{2,1,0:T(8,128)S(1)} %get-tuple-element.29, ...), kind=kLoop, calls=%fused_computation.127 | loop fusion | flops 23068672 | bytes 4194304 | tf_op jit(solution)/shard_map/broadcast_in_dim | solution.py:128
  80.3 3.5 %collective-permute-start.6 = (f32[4,2,32,256]{3,2,1,0:T(8,128)}, f32[4,2,32,256]{3,2,1,0:T(8,128)S(1)}, u32[]{:S(2)}, u32[]{:S(2)}) collective-permute-start(f32[4,2,32,256]{3,2,1,0:T(8,128)} %get-tuple-element.64), channel_id=1, source_target_pairs={{0,4},{4,8},{8,12},{1,5},{5,9},{9,13},{2,6},{6,10},{10,14},{3,7},{... | collective-permute-start | bytes 786440 | tf_op jit(solution)/shard_map/ppermute | solution.py:21
  85.7 4.3 %collective-permute-done.6 = f32[4,2,32,256]{3,2,1,0:T(8,128)S(1)} collective-permute-done((f32[4,2,32,256]{3,2,1,0:T(8,128)}, f32[4,2,32,256]{3,2,1,0:T(8,128)S(1)}, u32[]{:S(2)}, u32[]{:S(2)}) %collective-permute-start.6) | collective-permute-done | bytes 262176 | tf_op jit(solution)/shard_map/ppermute | solution.py:21
  90.0 4.7 %collective-permute-done.7 = f32[4,2,32,256]{3,2,1,0:T(8,128)} collective-permute-done((f32[4,2,32,256]{3,2,1,0:T(8,128)}, f32[4,2,32,256]{3,2,1,0:T(8,128)}, u32[]{:S(2)}, u32[]{:S(2)}) %collective-permute-start.7) | collective-permute-done | bytes 262176 | tf_op jit(solution)/shard_map/ppermute | solution.py:24
  100.0 4.1 %collective-permute-done.9 = f32[4,12,2,256]{3,2,1,0:T(2,128)S(1)} collective-permute-done((f32[4,12,2,256]{3,2,1,0:T(2,128)S(1)}, f32[4,12,2,256]{3,2,1,0:T(2,128)S(1)}, u32[]{:S(2)}, u32[]{:S(2)}) %collective-permute-start.9) | collective-permute-done | bytes 98336 | tf_op jit(solution)/shard_map/ppermute | solution.py:24
  108.8 1.9 collective-permute-start.10
  110.7 2.2 copy.29
  117.0 2.2 copy.30
  119.2 2.2 copy.31
  121.4 3.3 %pad_maximum_fusion.1 = f32[4,12,36,260]{3,2,1,0:T(8,128)S(1)} fusion(f32[4,12,36,2]{3,2,1,0:T(8,128)} %copy.31, f32[4,12,2,256]{3,2,1,0:T(2,128)} %copy-done.12, f32[4,2,32,256]{3,2,1,0:T(8,128)} %collective-permute-done.7, f32[1,8,32,256]{3,2,1,0:T(8,128)S(1)} %fusion.51, f32[3,8,32,256]{3,2,1,0:T(8,128)} %copy-done.2, ...), kind=kLoop, calls=%fused_computation.4 | loop fusion | flops 3144960 | bytes 3594240 | tf_op jit(solution)/shard_map/concatenate | solution.py:25
  124.9 3.8 %multiply_multiply_fusion.2 = (f32[10,34,258]{2,1,0:T(8,128)S(1)}, f32[10,34,258]{2,1,0:T(8,128)}, f32[10,34,258]{2,1,0:T(8,128)S(1)}, f32[10,34,258]{2,1,0:T(8,...) fusion(f32[12,36,260]{2,1,0:T(8,128)S(1)} %get-tuple-element.33, ...), kind=kLoop, calls=%fused_computation.61 | loop fusion | flops 2456160 | bytes 8421120 | tf_op jit(solution)/shard_map/mul | solution.py:106
  128.7 2.1 multiply_multiply_fusion
  135.0 60.5 %psum.7 = f32[3,4096]{1,0:T(4,128)} all-reduce(f32[3,4096]{1,0:T(4,128)} %fusion), channel_id=1, replica_groups=mesh['groups'=2,'slab'=4,'pencil'=2,'comp'=2] {'slab','pencil','comp'}, use_global_device_ids=true, to_apply=%region_1.0 | all-reduce | flops 12288 | bytes 98304 | tf_op jit(solution)/shard_map/psum | solution.py:144
  195.5 31.0 %fusion.26 = f32[8,32,256]{2,1,0:T(8,128)} fusion(f32[8,32,256]{2,1,0:T(8,128)} %param.6, f32[12,36,260]{2,1,0:T(8,128)S(1)} %copy-done.4, f32[10,34,258]{2,1,0:T(8,128)S(1)} %get-tuple-element.39, f32[10,34,258]{2,1,0:T(8,128)} %get-tuple-element.40, f32[10,34,258]{2,1,0:T(8,128)} %get-tuple-element.18, f32[10,34,258]{2,1,0:T(8,128)} %get-tuple-element.44, ...), kind=kLoop, calls=%fused_computation.82 | loop fusion | flops 23068672 | bytes 4194304 | tf_op jit(solution)/shard_map/add | solution.py:115
  (74 shorter events, 37.3 us)
Async XLA Ops:
  0.6 132.5 %copy-start = (bf16[8,32,1,4096]{3,1,2,0:T(8,128)(2,1)S(1)}, bf16[8,32,1,4096]{3,1,2,0:T(8,128)(2,1)}, u32[]{:S(2)}) copy-start(bf16[8,32,1,4096]{3,1,2,0:T(8,128)(2,1)} %param.8) | copy-start | bytes 6291460
  0.6 28.0 %copy-start.1 = (f32[3,8,32,256]{3,2,1,0:T(8,128)S(1)}, f32[3,8,32,256]{3,2,1,0:T(8,128)}, u32[]{:S(2)}) copy-start(f32[3,8,32,256]{3,2,1,0:T(8,128)} %param.5) | copy-start | bytes 2359300
  2.9 10.5 %collective-permute-start = (f32[4,2,32,256]{3,2,1,0:T(8,128)S(1)}, f32[4,2,32,256]{3,2,1,0:T(8,128)S(1)}, u32[]{:S(2)}, u32[]{:S(2)}) collective-permute-start(f32[4,2,32,256]{3,2,1,0:T(8,128)S(1)} %get-tuple-element.66), channel_id=1, source_target_pairs={{0,4},{4,8},{8,12},{1,5},{5,9},{9,13},{2,6},{6,10},{10,14},{3,7},{... | collective-permute-start | bytes 786440 | tf_op jit(solution)/shard_map/ppermute | solution.py:21
  7.8 9.7 %collective-permute-start.1 = (f32[4,2,32,256]{3,2,1,0:T(8,128)S(1)}, f32[4,2,32,256]{3,2,1,0:T(8,128)S(1)}, u32[]{:S(2)}, u32[]{:S(2)}) collective-permute-start(f32[4,2,32,256]{3,2,1,0:T(8,128)S(1)} %get-tuple-element.67), channel_id=1, source_target_pairs={{4,0},{8,4},{12,8},{5,1},{9,5},{13,9},{6,2},{10,6},{14,10},{7,3},{... | collective-permute-start | bytes 786440 | tf_op jit(solution)/shard_map/ppermute | solution.py:24
  17.5 13.0 %copy-start.5 = (f32[4,2,32,256]{3,2,1,0:T(8,128)}, f32[4,2,32,256]{3,2,1,0:T(8,128)S(1)}, u32[]{:S(2)}) copy-start(f32[4,2,32,256]{3,2,1,0:T(8,128)S(1)} %collective-permute-done.1) | copy-start | bytes 786436
  18.7 5.6 %collective-permute-start.2 = (f32[4,12,2,256]{3,2,1,0:T(2,128)S(1)}, f32[4,12,2,256]{3,2,1,0:T(2,128)S(1)}, u32[]{:S(2)}, u32[]{:S(2)}) collective-permute-start(f32[4,12,2,256]{3,2,1,0:T(2,128)S(1)} %get-tuple-element.58), channel_id=1, source_target_pairs={{0,2},{1,3},{4,6},{5,7},{8,10},{9,11},{12,14},{13,15},{16,18},{17,... | collective-permute-start | bytes 294920 | tf_op jit(solution)/shard_map/ppermute | solution.py:21
  22.1 6.5 %collective-permute-start.3 = (f32[4,12,2,256]{3,2,1,0:T(2,128)S(1)}, f32[4,12,2,256]{3,2,1,0:T(2,128)S(1)}, u32[]{:S(2)}, u32[]{:S(2)}) collective-permute-start(f32[4,12,2,256]{3,2,1,0:T(2,128)S(1)} %get-tuple-element.59), channel_id=1, source_target_pairs={{2,0},{3,1},{6,4},{7,5},{10,8},{11,9},{14,12},{15,13},{18,16},{19,... | collective-permute-start | bytes 294920 | tf_op jit(solution)/shard_map/ppermute | solution.py:24
  28.6 1.9 copy-start.13
  32.2 5.4 %collective-permute-start.4 = (f32[4,12,36,2]{2,0,3,1:T(4,128)S(1)}, f32[4,12,36,2]{2,0,3,1:T(4,128)}, u32[]{:S(2)}, u32[]{:S(2)}) collective-permute-start(f32[4,12,36,2]{2,0,3,1:T(4,128)S(1)} %copy.24), channel_id=1, source_target_pairs={{0,1},{2,3},{4,5},{6,7},{8,9},{10,11},{12,13},{14,15},{16,17},{18,... | collective-permute-start | bytes 41480 | tf_op jit(solution)/shard_map/ppermute | solution.py:21
  36.3 3.5 %collective-permute-start.5 = (f32[4,12,36,2]{2,0,3,1:T(4,128)}, f32[4,12,36,2]{2,0,3,1:T(4,128)}, u32[]{:S(2)}, u32[]{:S(2)}) collective-permute-start(f32[4,12,36,2]{2,0,3,1:T(4,128)} %copy.25), channel_id=1, source_target_pairs={{1,0},{3,2},{5,4},{7,6},{9,8},{11,10},{13,12},{15,14},{17,16},{19,... | collective-permute-start | bytes 41480 | tf_op jit(solution)/shard_map/ppermute | solution.py:24
  49.9 29.5 %copy-start.6 = (f32[1,8,32,256]{3,2,1,0:T(8,128)}, f32[1,8,32,256]{3,2,1,0:T(8,128)S(1)}, u32[]{:S(2)}) copy-start(f32[1,8,32,256]{3,2,1,0:T(8,128)S(1)} %get-tuple-element.71) | copy-start | bytes 786436
  49.9 29.5 %copy-start.8 = (f32[1,8,32,256]{3,2,1,0:T(8,128)}, f32[1,8,32,256]{3,2,1,0:T(8,128)S(1)}, u32[]{:S(2)}) copy-start(f32[1,8,32,256]{3,2,1,0:T(8,128)S(1)} %get-tuple-element.72) | copy-start | bytes 786436
  50.0 29.5 %copy-start.10 = (f32[1,8,32,256]{3,2,1,0:T(8,128)}, f32[1,8,32,256]{3,2,1,0:T(8,128)S(1)}, u32[]{:S(2)}) copy-start(f32[1,8,32,256]{3,2,1,0:T(8,128)S(1)} %get-tuple-element.73) | copy-start | bytes 786436
  50.1 30.2 %copy-start.2 = (f32[3,8,32,256]{3,2,1,0:T(8,128)}, f32[3,8,32,256]{3,2,1,0:T(8,128)S(1)}, u32[]{:S(2)}) copy-start(f32[3,8,32,256]{3,2,1,0:T(8,128)S(1)} %fusion.4) | copy-start | bytes 2359300
  80.3 9.7 %collective-permute-start.6 = (f32[4,2,32,256]{3,2,1,0:T(8,128)}, f32[4,2,32,256]{3,2,1,0:T(8,128)S(1)}, u32[]{:S(2)}, u32[]{:S(2)}) collective-permute-start(f32[4,2,32,256]{3,2,1,0:T(8,128)} %get-tuple-element.64), channel_id=1, source_target_pairs={{0,4},{4,8},{8,12},{1,5},{5,9},{9,13},{2,6},{6,10},{10,14},{3,7},{... | collective-permute-start | bytes 786440 | tf_op jit(solution)/shard_map/ppermute | solution.py:21
  83.8 10.9 %collective-permute-start.7 = (f32[4,2,32,256]{3,2,1,0:T(8,128)}, f32[4,2,32,256]{3,2,1,0:T(8,128)}, u32[]{:S(2)}, u32[]{:S(2)}) collective-permute-start(f32[4,2,32,256]{3,2,1,0:T(8,128)} %get-tuple-element.65), channel_id=1, source_target_pairs={{4,0},{8,4},{12,8},{5,1},{9,5},{13,9},{6,2},{10,6},{14,10},{7,3},{... | collective-permute-start | bytes 786440 | tf_op jit(solution)/shard_map/ppermute | solution.py:24
  95.9 4.1 %collective-permute-start.8 = (f32[4,12,2,256]{3,2,1,0:T(2,128)S(1)}, f32[4,12,2,256]{3,2,1,0:T(2,128)S(1)}, u32[]{:S(2)}, u32[]{:S(2)}) collective-permute-start(f32[4,12,2,256]{3,2,1,0:T(2,128)S(1)} %get-tuple-element.56), channel_id=1, source_target_pairs={{0,2},{1,3},{4,6},{5,7},{8,10},{9,11},{12,14},{13,15},{16,18},{17,... | collective-permute-start | bytes 294920 | tf_op jit(solution)/shard_map/ppermute | solution.py:21
  97.4 6.7 %collective-permute-start.9 = (f32[4,12,2,256]{3,2,1,0:T(2,128)S(1)}, f32[4,12,2,256]{3,2,1,0:T(2,128)S(1)}, u32[]{:S(2)}, u32[]{:S(2)}) collective-permute-start(f32[4,12,2,256]{3,2,1,0:T(2,128)S(1)} %get-tuple-element.57), channel_id=1, source_target_pairs={{2,0},{3,1},{6,4},{7,5},{10,8},{11,9},{14,12},{15,13},{18,16},{19,... | collective-permute-start | bytes 294920 | tf_op jit(solution)/shard_map/ppermute | solution.py:24
  104.1 3.1 %copy-start.12 = (f32[4,12,2,256]{3,2,1,0:T(2,128)}, f32[4,12,2,256]{3,2,1,0:T(2,128)S(1)}, u32[]{:S(2)}) copy-start(f32[4,12,2,256]{3,2,1,0:T(2,128)S(1)} %collective-permute-done.9) | copy-start | bytes 294916
  108.8 8.1 %collective-permute-start.10 = (f32[4,12,36,2]{2,0,3,1:T(4,128)S(1)}, f32[4,12,36,2]{2,0,3,1:T(4,128)}, u32[]{:S(2)}, u32[]{:S(2)}) collective-permute-start(f32[4,12,36,2]{2,0,3,1:T(4,128)S(1)} %copy.28), channel_id=1, source_target_pairs={{0,1},{2,3},{4,5},{6,7},{8,9},{10,11},{12,13},{14,15},{16,17},{18,... | collective-permute-start | bytes 41480 | tf_op jit(solution)/shard_map/ppermute | solution.py:21
  113.0 6.2 %collective-permute-start.11 = (f32[4,12,36,2]{2,0,3,1:T(4,128)}, f32[4,12,36,2]{2,0,3,1:T(4,128)}, u32[]{:S(2)}, u32[]{:S(2)}) collective-permute-start(f32[4,12,36,2]{2,0,3,1:T(4,128)} %copy.29), channel_id=1, source_target_pairs={{1,0},{3,2},{5,4},{7,6},{9,8},{11,10},{13,12},{15,14},{17,16},{19,... | collective-permute-start | bytes 41480 | tf_op jit(solution)/shard_map/ppermute | solution.py:24
  124.9 3.8 %copy-start.3 = (f32[12,36,260]{2,1,0:T(8,128)}, f32[12,36,260]{2,1,0:T(8,128)S(1)}, u32[]{:S(2)}) copy-start(f32[12,36,260]{2,1,0:T(8,128)S(1)} %get-tuple-element.33) | copy-start | bytes 1347844
  132.0 1.6 copy-start.14
  133.1 62.5 %copy-start.4 = (f32[12,36,260]{2,1,0:T(8,128)S(1)}, f32[12,36,260]{2,1,0:T(8,128)}, u32[]{:S(2)}) copy-start(f32[12,36,260]{2,1,0:T(8,128)} %copy-done.3) | copy-start | bytes 1347844
  (5 other events, 6.4 us)
where the time goes:
time: 228 us; the launch traced here: 227 us
  other arithmetic  89.2 us (39%)
  blocking collectives  60.5 us (27%)
  waiting for transfers between devices  27.4 us (12%)
  starting transfers between devices  24.9 us (11%)
  local copies, waits for them, and re-layouts  21.7 us (10%)
    psum x1, blocking collectives, local(): readings = lax.psum(partial_sum, ('slab', 'pencil', 'comp'))  60.5 us
    add x1, other arithmetic, advance(): damage_core + TIME_DAMAGE * (2.0 * (1.0 - damage_core) * energy - toughne...  31 us
    broadcast_in_dim x2, other arithmetic, local(): stacked = jnp.concatenate([moved, damage[None]], axis=0)  30.5 us
    ppermute x6, waiting for transfers between devices, with_halo(): lax.ppermute(lax.slice_in_dim(block, 0, width, axis=dim), axis, backward)  17.3 us
    ppermute x6, starting transfers between devices, with_halo(): lax.ppermute(lax.slice_in_dim(block, block.shape[dim] - width, None, axis...  17.2 us
    ppermute x6, waiting for transfers between devices, with_halo(): lax.ppermute(lax.slice_in_dim(block, block.shape[dim] - width, None, axis...  10.2 us
    mul x4, other arithmetic, advance(): total_force = total_force + central(degrade * stress, direction)  9.3 us
    concatenate x4, other arithmetic, with_halo(): block = jnp.concatenate([low, block, high], axis=dim)  8.23 us
  transfers between devices with their start and end apart: 12, of which 8 were waited for; matrix products, arithmetic and copies ran while one was open for 6% of the time, Pallas kernels for 0%

commit v1 on v0

--- a/solution.py
+++ b/solution.py
@@ -141,7 +141,7 @@
     picks = (block_ids[:, None] == sensor_cell[None, :]).astype(jnp.bfloat16)
     point = jnp.dot(pooled, picks, preferred_element_type=jnp.float32)
     partial_sum = dense + POINT_GAIN * point
-    readings = lax.psum(partial_sum, ("slab", "pencil", "comp"))
+    readings = lax.psum(lax.psum(partial_sum, ("pencil", "comp")), "slab")
     return (moved, damage, readings)
 
 

time: 228 us -> 199 us (0.87)
  blocking collectives: 60.5 us -> 32.4 us
    psum x1 -> x2, blocking collectives: 60.5 us -> 32.4 us  [local(): readings = lax.psum(lax.psum(partial_sum, ('pencil', 'comp')), 'slab')]
where the time goes in v1:
time: 199 us; the launch traced here: 198 us
  other arithmetic  89.2 us (45%)
  blocking collectives  32.4 us (16%)
  waiting for transfers between devices  27.4 us (14%)
  starting transfers between devices  24.9 us (13%)
  local copies, waits for them, and re-layouts  21.6 us (11%)
    psum x2, blocking collectives, local(): readings = lax.psum(lax.psum(partial_sum, ('pencil', 'comp')), 'slab')  32.4 us
    add x1, other arithmetic, advance(): damage_core + TIME_DAMAGE * (2.0 * (1.0 - damage_core) * energy - toughne...  31 us
    broadcast_in_dim x2, other arithmetic, local(): stacked = jnp.concatenate([moved, damage[None]], axis=0)  30.5 us
    ppermute x6, waiting for transfers between devices, with_halo(): lax.ppermute(lax.slice_in_dim(block, 0, width, axis=dim), axis, backward)  17.3 us
    ppermute x6, starting transfers between devices, with_halo(): lax.ppermute(lax.slice_in_dim(block, block.shape[dim] - width, None, axis...  17.2 us
    ppermute x6, waiting for transfers between devices, with_halo(): lax.ppermute(lax.slice_in_dim(block, block.shape[dim] - width, None, axis...  10.2 us
    mul x4, other arithmetic, advance(): total_force = total_force + central(degrade * stress, direction)  9.29 us
    concatenate x4, other arithmetic, with_halo(): block = jnp.concatenate([low, block, high], axis=dim)  8.23 us
  transfers between devices with their start and end apart: 12, of which 8 were waited for; matrix products, arithmetic and copies ran while one was open for 6% of the time, Pallas kernels for 0%

profile of v1, /device:TPU:0, one launch (start us, length us, event | category | flops | bytes accessed | tf_op | source)
XLA Modules:
  0.0 198.3 jit_solution(6392103848237153128)
XLA Ops:
  2.9 5.0 %collective-permute-start = (f32[4,2,32,256]{3,2,1,0:T(8,128)S(1)}, f32[4,2,32,256]{3,2,1,0:T(8,128)S(1)}, u32[]{:S(2)}, u32[]{:S(2)}) collective-permute-start(f32[4,2,32,256]{3,2,1,0:T(8,128)S(1)} %get-tuple-element.66), channel_id=1, source_target_pairs={{0,4},{4,8},{8,12},{1,5},{5,9},{9,13},{2,6},{6,10},{10,14},{3,7},{... | collective-permute-start | bytes 786440 | tf_op jit(solution)/shard_map/ppermute | solution.py:21
  9.1 4.2 %collective-permute-done = f32[4,2,32,256]{3,2,1,0:T(8,128)S(1)} collective-permute-done((f32[4,2,32,256]{3,2,1,0:T(8,128)S(1)}, f32[4,2,32,256]{3,2,1,0:T(8,128)S(1)}, u32[]{:S(2)}, u32[]{:S(2)}) %collective-permute-start) | collective-permute-done | bytes 262176 | tf_op jit(solution)/shard_map/ppermute | solution.py:21
  13.4 4.1 %collective-permute-done.1 = f32[4,2,32,256]{3,2,1,0:T(8,128)S(1)} collective-permute-done((f32[4,2,32,256]{3,2,1,0:T(8,128)S(1)}, f32[4,2,32,256]{3,2,1,0:T(8,128)S(1)}, u32[]{:S(2)}, u32[]{:S(2)}) %collective-permute-start.1) | collective-permute-done | bytes 262176 | tf_op jit(solution)/shard_map/ppermute | solution.py:24
  18.7 3.4 %collective-permute-start.2 = (f32[4,12,2,256]{3,2,1,0:T(2,128)S(1)}, f32[4,12,2,256]{3,2,1,0:T(2,128)S(1)}, u32[]{:S(2)}, u32[]{:S(2)}) collective-permute-start(f32[4,12,2,256]{3,2,1,0:T(2,128)S(1)} %get-tuple-element.58), channel_id=1, source_target_pairs={{0,2},{1,3},{4,6},{5,7},{8,10},{9,11},{12,14},{13,15},{16,18},{17,... | collective-permute-start | bytes 294920 | tf_op jit(solution)/shard_map/ppermute | solution.py:21
  24.3 4.3 %collective-permute-done.3 = f32[4,12,2,256]{3,2,1,0:T(2,128)S(1)} collective-permute-done((f32[4,12,2,256]{3,2,1,0:T(2,128)S(1)}, f32[4,12,2,256]{3,2,1,0:T(2,128)S(1)}, u32[]{:S(2)}, u32[]{:S(2)}) %collective-permute-start.3) | collective-permute-done | bytes 98336 | tf_op jit(solution)/shard_map/ppermute | solution.py:24
  34.0 2.2 %copy.25 = f32[4,12,36,2]{2,0,3,1:T(4,128)} copy(f32[4,12,36,2]{3,2,1,0:T(8,128)} %get-tuple-element.55) | data formatting | bytes 27648 | tf_op jit(solution)/shard_map/slice | solution.py:24
  37.6 2.2 %copy.26 = f32[4,12,36,2]{3,2,1,0:T(8,128)} copy(f32[4,12,36,2]{2,0,3,1:T(4,128)} %collective-permute-done.4) | data formatting | bytes 27648 | tf_op jit(solution)/shard_map/ppermute | solution.py:21
  39.8 2.2 %copy.27 = f32[4,12,36,2]{3,2,1,0:T(8,128)} copy(f32[4,12,36,2]{2,0,3,1:T(4,128)} %collective-permute-done.5) | data formatting | bytes 27648 | tf_op jit(solution)/shard_map/ppermute | solution.py:24
  42.0 3.1 %pad_maximum_fusion = f32[4,12,36,260]{3,2,1,0:T(8,128)S(1)} fusion(f32[4,12,36,2]{3,2,1,0:T(8,128)} %copy.27, f32[4,12,2,256]{3,2,1,0:T(2,128)} %copy-done.13, f32[4,2,32,256]{3,2,1,0:T(8,128)} %copy-done.5, f32[1,8,32,256]{3,2,1,0:T(8,128)S(1)} %multiply_bitcast_fusion, f32[3,8,32,256]{3,2,1,0:T(8,128)S(1)} %copy-done.1, ...), kind=kLoop, calls=%fused_computation.3 | loop fusion | flops 3144960 | bytes 3594240 | tf_op jit(solution)/shard_map/concatenate | solution.py:25
  45.3 2.2 %multiply_multiply_fusion.5 = (f32[10,34,258]{2,1,0:T(8,128)S(1)}, f32[10,34,258]{2,1,0:T(8,128)S(1)}, f32[10,34,258]{2,1,0:T(8,128)S(1)}, f32[10,34,258]{2,1,0:...) fusion(f32[12,36,260]{2,1,0:T(8,128)S(1)} %get-tuple-element.37, ...), kind=kLoop, calls=%fused_computation.68 | loop fusion | flops 2456160 | bytes 8421120 | tf_op jit(solution)/shard_map/mul | solution.py:106
  50.1 29.3 %fusion.51 = f32[1,8,32,256]{3,2,1,0:T(8,128)S(1)} fusion(f32[8,32,256]{2,1,0:T(8,128)S(1)} %copy-done.15, f32[12,36,260]{2,1,0:T(8,128)S(1)} %get-tuple-element.37, f32[10,34,258]{2,1,0:T(8,128)S(1)} %get-tuple-element.46, f32[10,34,258]{2,1,0:T(8,128)S(1)} %get-tuple-element.47, f32[10,34,258]{2,1,0:T(8,128)S(1)} %get-tuple-element.29, ...), kind=kLoop, calls=%fused_computation.127 | loop fusion | flops 23068672 | bytes 4194304 | tf_op jit(solution)/shard_map/broadcast_in_dim | solution.py:128
  80.3 3.5 %collective-permute-start.6 = (f32[4,2,32,256]{3,2,1,0:T(8,128)}, f32[4,2,32,256]{3,2,1,0:T(8,128)S(1)}, u32[]{:S(2)}, u32[]{:S(2)}) collective-permute-start(f32[4,2,32,256]{3,2,1,0:T(8,128)} %get-tuple-element.64), channel_id=1, source_target_pairs={{0,4},{4,8},{8,12},{1,5},{5,9},{9,13},{2,6},{6,10},{10,14},{3,7},{... | collective-permute-start | bytes 786440 | tf_op jit(solution)/shard_map/ppermute | solution.py:21
  85.6 4.4 %collective-permute-done.6 = f32[4,2,32,256]{3,2,1,0:T(8,128)S(1)} collective-permute-done((f32[4,2,32,256]{3,2,1,0:T(8,128)}, f32[4,2,32,256]{3,2,1,0:T(8,128)S(1)}, u32[]{:S(2)}, u32[]{:S(2)}) %collective-permute-start.6) | collective-permute-done | bytes 262176 | tf_op jit(solution)/shard_map/ppermute | solution.py:21
  90.0 4.7 %collective-permute-done.7 = f32[4,2,32,256]{3,2,1,0:T(8,128)} collective-permute-done((f32[4,2,32,256]{3,2,1,0:T(8,128)}, f32[4,2,32,256]{3,2,1,0:T(8,128)}, u32[]{:S(2)}, u32[]{:S(2)}) %collective-permute-start.7) | collective-permute-done | bytes 262176 | tf_op jit(solution)/shard_map/ppermute | solution.py:24
  99.9 4.1 %collective-permute-done.9 = f32[4,12,2,256]{3,2,1,0:T(2,128)S(1)} collective-permute-done((f32[4,12,2,256]{3,2,1,0:T(2,128)S(1)}, f32[4,12,2,256]{3,2,1,0:T(2,128)S(1)}, u32[]{:S(2)}, u32[]{:S(2)}) %collective-permute-start.9) | collective-permute-done | bytes 98336 | tf_op jit(solution)/shard_map/ppermute | solution.py:24
  110.7 2.2 %copy.29 = f32[4,12,36,2]{2,0,3,1:T(4,128)} copy(f32[4,12,36,2]{3,2,1,0:T(8,128)} %get-tuple-element.53) | data formatting | bytes 27648 | tf_op jit(solution)/shard_map/slice | solution.py:24
  116.8 2.2 %copy.30 = f32[4,12,36,2]{3,2,1,0:T(8,128)} copy(f32[4,12,36,2]{2,0,3,1:T(4,128)} %collective-permute-done.10) | data formatting | bytes 27648 | tf_op jit(solution)/shard_map/ppermute | solution.py:21
  119.1 2.2 %copy.31 = f32[4,12,36,2]{3,2,1,0:T(8,128)} copy(f32[4,12,36,2]{2,0,3,1:T(4,128)} %collective-permute-done.11) | data formatting | bytes 27648 | tf_op jit(solution)/shard_map/ppermute | solution.py:24
  121.2 3.3 %pad_maximum_fusion.1 = f32[4,12,36,260]{3,2,1,0:T(8,128)S(1)} fusion(f32[4,12,36,2]{3,2,1,0:T(8,128)} %copy.31, f32[4,12,2,256]{3,2,1,0:T(2,128)} %copy-done.12, f32[4,2,32,256]{3,2,1,0:T(8,128)} %collective-permute-done.7, f32[1,8,32,256]{3,2,1,0:T(8,128)S(1)} %fusion.51, f32[3,8,32,256]{3,2,1,0:T(8,128)} %copy-done.2, ...), kind=kLoop, calls=%fused_computation.4 | loop fusion | flops 3144960 | bytes 3594240 | tf_op jit(solution)/shard_map/concatenate | solution.py:25
  124.8 3.8 %multiply_multiply_fusion.2 = (f32[10,34,258]{2,1,0:T(8,128)S(1)}, f32[10,34,258]{2,1,0:T(8,128)}, f32[10,34,258]{2,1,0:T(8,128)S(1)}, f32[10,34,258]{2,1,0:T(8,...) fusion(f32[12,36,260]{2,1,0:T(8,128)S(1)} %get-tuple-element.33, ...), kind=kLoop, calls=%fused_computation.61 | loop fusion | flops 2456160 | bytes 8421120 | tf_op jit(solution)/shard_map/mul | solution.py:106
  128.6 2.1 %multiply_multiply_fusion = (f32[10,34,258]{2,1,0:T(8,128)S(1)}, f32[10,34,258]{2,1,0:T(8,128)}, f32[10,34,258]{2,1,0:T(8,128)S(1)}, f32[10,34,258]{2,1,0:T(8,128)S(1)}) fusion(f32[12,36,260]{2,1,0:T(8,128)S(1)} %get-tuple-element.33, f32[12,36,260]{2,1,0:T(8,128)S(1)} %get-tuple-element.30, f32[12,36,260]{2,1,0:T(8,128)S(1)} %get-tuple-element.31, ...), kind=kLoop, calls=%fused_computation.58 | loop fusion | flops 1666680 | bytes 4912320 | tf_op jit(solution)/shard_map/mul | solution.py:106
  134.8 13.5 %psum.14 = f32[3,4096]{1,0:T(4,128)} all-reduce(f32[3,4096]{1,0:T(4,128)} %fusion), channel_id=1, replica_groups=mesh['groups'=2,'slab'=4,'pencil'=2,'comp'=2] {'pencil','comp'}, use_global_device_ids=true, to_apply=%region_1.0 | all-reduce | flops 12288 | bytes 98304 | tf_op jit(solution)/shard_map/psum | solution.py:144
  148.3 19.0 %psum.15 = f32[3,4096]{1,0:T(4,128)} all-reduce(f32[3,4096]{1,0:T(4,128)} %psum.14), channel_id=1, replica_groups=mesh['groups'=2,'slab'=4,'pencil'=2,'comp'=2] {'slab'}, use_global_device_ids=true, to_apply=%region_2.0 | all-reduce | flops 12288 | bytes 98304 | tf_op jit(solution)/shard_map/psum | solution.py:144
  167.3 31.0 %fusion.26 = f32[8,32,256]{2,1,0:T(8,128)} fusion(f32[8,32,256]{2,1,0:T(8,128)} %param.6, f32[12,36,260]{2,1,0:T(8,128)S(1)} %copy-done.4, f32[10,34,258]{2,1,0:T(8,128)S(1)} %get-tuple-element.39, f32[10,34,258]{2,1,0:T(8,128)} %get-tuple-element.40, f32[10,34,258]{2,1,0:T(8,128)} %get-tuple-element.18, f32[10,34,258]{2,1,0:T(8,128)} %get-tuple-element.44, ...), kind=kLoop, calls=%fused_computation.82 | loop fusion | flops 23068672 | bytes 4194304 | tf_op jit(solution)/shard_map/add | solution.py:115
  (75 shorter events, 39.0 us)
Async XLA Ops:
  0.6 132.4 %copy-start = (bf16[8,32,1,4096]{3,1,2,0:T(8,128)(2,1)S(1)}, bf16[8,32,1,4096]{3,1,2,0:T(8,128)(2,1)}, u32[]{:S(2)}) copy-start(bf16[8,32,1,4096]{3,1,2,0:T(8,128)(2,1)} %param.8) | copy-start | bytes 6291460
  0.6 28.0 %copy-start.1 = (f32[3,8,32,256]{3,2,1,0:T(8,128)S(1)}, f32[3,8,32,256]{3,2,1,0:T(8,128)}, u32[]{:S(2)}) copy-start(f32[3,8,32,256]{3,2,1,0:T(8,128)} %param.5) | copy-start | bytes 2359300
  2.9 10.5 %collective-permute-start = (f32[4,2,32,256]{3,2,1,0:T(8,128)S(1)}, f32[4,2,32,256]{3,2,1,0:T(8,128)S(1)}, u32[]{:S(2)}, u32[]{:S(2)}) collective-permute-start(f32[4,2,32,256]{3,2,1,0:T(8,128)S(1)} %get-tuple-element.66), channel_id=1, source_target_pairs={{0,4},{4,8},{8,12},{1,5},{5,9},{9,13},{2,6},{6,10},{10,14},{3,7},{... | collective-permute-start | bytes 786440 | tf_op jit(solution)/shard_map/ppermute | solution.py:21
  7.8 9.7 %collective-permute-start.1 = (f32[4,2,32,256]{3,2,1,0:T(8,128)S(1)}, f32[4,2,32,256]{3,2,1,0:T(8,128)S(1)}, u32[]{:S(2)}, u32[]{:S(2)}) collective-permute-start(f32[4,2,32,256]{3,2,1,0:T(8,128)S(1)} %get-tuple-element.67), channel_id=1, source_target_pairs={{4,0},{8,4},{12,8},{5,1},{9,5},{13,9},{6,2},{10,6},{14,10},{7,3},{... | collective-permute-start | bytes 786440 | tf_op jit(solution)/shard_map/ppermute | solution.py:24
  17.5 13.0 %copy-start.5 = (f32[4,2,32,256]{3,2,1,0:T(8,128)}, f32[4,2,32,256]{3,2,1,0:T(8,128)S(1)}, u32[]{:S(2)}) copy-start(f32[4,2,32,256]{3,2,1,0:T(8,128)S(1)} %collective-permute-done.1) | copy-start | bytes 786436
  18.7 5.6 %collective-permute-start.2 = (f32[4,12,2,256]{3,2,1,0:T(2,128)S(1)}, f32[4,12,2,256]{3,2,1,0:T(2,128)S(1)}, u32[]{:S(2)}, u32[]{:S(2)}) collective-permute-start(f32[4,12,2,256]{3,2,1,0:T(2,128)S(1)} %get-tuple-element.58), channel_id=1, source_target_pairs={{0,2},{1,3},{4,6},{5,7},{8,10},{9,11},{12,14},{13,15},{16,18},{17,... | collective-permute-start | bytes 294920 | tf_op jit(solution)/shard_map/ppermute | solution.py:21
  22.1 6.5 %collective-permute-start.3 = (f32[4,12,2,256]{3,2,1,0:T(2,128)S(1)}, f32[4,12,2,256]{3,2,1,0:T(2,128)S(1)}, u32[]{:S(2)}, u32[]{:S(2)}) collective-permute-start(f32[4,12,2,256]{3,2,1,0:T(2,128)S(1)} %get-tuple-element.59), channel_id=1, source_target_pairs={{2,0},{3,1},{6,4},{7,5},{10,8},{11,9},{14,12},{15,13},{18,16},{19,... | collective-permute-start | bytes 294920 | tf_op jit(solution)/shard_map/ppermute | solution.py:24
  28.6 1.9 copy-start.13
  32.1 5.4 %collective-permute-start.4 = (f32[4,12,36,2]{2,0,3,1:T(4,128)S(1)}, f32[4,12,36,2]{2,0,3,1:T(4,128)}, u32[]{:S(2)}, u32[]{:S(2)}) collective-permute-start(f32[4,12,36,2]{2,0,3,1:T(4,128)S(1)} %copy.24), channel_id=1, source_target_pairs={{0,1},{2,3},{4,5},{6,7},{8,9},{10,11},{12,13},{14,15},{16,17},{18,... | collective-permute-start | bytes 41480 | tf_op jit(solution)/shard_map/ppermute | solution.py:21
  36.3 3.5 %collective-permute-start.5 = (f32[4,12,36,2]{2,0,3,1:T(4,128)}, f32[4,12,36,2]{2,0,3,1:T(4,128)}, u32[]{:S(2)}, u32[]{:S(2)}) collective-permute-start(f32[4,12,36,2]{2,0,3,1:T(4,128)} %copy.25), channel_id=1, source_target_pairs={{1,0},{3,2},{5,4},{7,6},{9,8},{11,10},{13,12},{15,14},{17,16},{19,... | collective-permute-start | bytes 41480 | tf_op jit(solution)/shard_map/ppermute | solution.py:24
  49.9 29.5 %copy-start.6 = (f32[1,8,32,256]{3,2,1,0:T(8,128)}, f32[1,8,32,256]{3,2,1,0:T(8,128)S(1)}, u32[]{:S(2)}) copy-start(f32[1,8,32,256]{3,2,1,0:T(8,128)S(1)} %get-tuple-element.71) | copy-start | bytes 786436
  49.9 29.5 %copy-start.8 = (f32[1,8,32,256]{3,2,1,0:T(8,128)}, f32[1,8,32,256]{3,2,1,0:T(8,128)S(1)}, u32[]{:S(2)}) copy-start(f32[1,8,32,256]{3,2,1,0:T(8,128)S(1)} %get-tuple-element.72) | copy-start | bytes 786436
  49.9 29.5 %copy-start.10 = (f32[1,8,32,256]{3,2,1,0:T(8,128)}, f32[1,8,32,256]{3,2,1,0:T(8,128)S(1)}, u32[]{:S(2)}) copy-start(f32[1,8,32,256]{3,2,1,0:T(8,128)S(1)} %get-tuple-element.73) | copy-start | bytes 786436
  50.1 30.2 %copy-start.2 = (f32[3,8,32,256]{3,2,1,0:T(8,128)}, f32[3,8,32,256]{3,2,1,0:T(8,128)S(1)}, u32[]{:S(2)}) copy-start(f32[3,8,32,256]{3,2,1,0:T(8,128)S(1)} %fusion.4) | copy-start | bytes 2359300
  80.3 9.7 %collective-permute-start.6 = (f32[4,2,32,256]{3,2,1,0:T(8,128)}, f32[4,2,32,256]{3,2,1,0:T(8,128)S(1)}, u32[]{:S(2)}, u32[]{:S(2)}) collective-permute-start(f32[4,2,32,256]{3,2,1,0:T(8,128)} %get-tuple-element.64), channel_id=1, source_target_pairs={{0,4},{4,8},{8,12},{1,5},{5,9},{9,13},{2,6},{6,10},{10,14},{3,7},{... | collective-permute-start | bytes 786440 | tf_op jit(solution)/shard_map/ppermute | solution.py:21
  83.8 10.9 %collective-permute-start.7 = (f32[4,2,32,256]{3,2,1,0:T(8,128)}, f32[4,2,32,256]{3,2,1,0:T(8,128)}, u32[]{:S(2)}, u32[]{:S(2)}) collective-permute-start(f32[4,2,32,256]{3,2,1,0:T(8,128)} %get-tuple-element.65), channel_id=1, source_target_pairs={{4,0},{8,4},{12,8},{5,1},{9,5},{13,9},{6,2},{10,6},{14,10},{7,3},{... | collective-permute-start | bytes 786440 | tf_op jit(solution)/shard_map/ppermute | solution.py:24
  95.8 4.1 %collective-permute-start.8 = (f32[4,12,2,256]{3,2,1,0:T(2,128)S(1)}, f32[4,12,2,256]{3,2,1,0:T(2,128)S(1)}, u32[]{:S(2)}, u32[]{:S(2)}) collective-permute-start(f32[4,12,2,256]{3,2,1,0:T(2,128)S(1)} %get-tuple-element.56), channel_id=1, source_target_pairs={{0,2},{1,3},{4,6},{5,7},{8,10},{9,11},{12,14},{13,15},{16,18},{17,... | collective-permute-start | bytes 294920 | tf_op jit(solution)/shard_map/ppermute | solution.py:21
  97.4 6.7 %collective-permute-start.9 = (f32[4,12,2,256]{3,2,1,0:T(2,128)S(1)}, f32[4,12,2,256]{3,2,1,0:T(2,128)S(1)}, u32[]{:S(2)}, u32[]{:S(2)}) collective-permute-start(f32[4,12,2,256]{3,2,1,0:T(2,128)S(1)} %get-tuple-element.57), channel_id=1, source_target_pairs={{2,0},{3,1},{6,4},{7,5},{10,8},{11,9},{14,12},{15,13},{18,16},{19,... | collective-permute-start | bytes 294920 | tf_op jit(solution)/shard_map/ppermute | solution.py:24
  104.0 3.1 %copy-start.12 = (f32[4,12,2,256]{3,2,1,0:T(2,128)}, f32[4,12,2,256]{3,2,1,0:T(2,128)S(1)}, u32[]{:S(2)}) copy-start(f32[4,12,2,256]{3,2,1,0:T(2,128)S(1)} %collective-permute-done.9) | copy-start | bytes 294916
  108.8 8.1 %collective-permute-start.10 = (f32[4,12,36,2]{2,0,3,1:T(4,128)S(1)}, f32[4,12,36,2]{2,0,3,1:T(4,128)}, u32[]{:S(2)}, u32[]{:S(2)}) collective-permute-start(f32[4,12,36,2]{2,0,3,1:T(4,128)S(1)} %copy.28), channel_id=1, source_target_pairs={{0,1},{2,3},{4,5},{6,7},{8,9},{10,11},{12,13},{14,15},{16,17},{18,... | collective-permute-start | bytes 41480 | tf_op jit(solution)/shard_map/ppermute | solution.py:21
  112.9 6.1 %collective-permute-start.11 = (f32[4,12,36,2]{2,0,3,1:T(4,128)}, f32[4,12,36,2]{2,0,3,1:T(4,128)}, u32[]{:S(2)}, u32[]{:S(2)}) collective-permute-start(f32[4,12,36,2]{2,0,3,1:T(4,128)} %copy.29), channel_id=1, source_target_pairs={{1,0},{3,2},{5,4},{7,6},{9,8},{11,10},{13,12},{15,14},{17,16},{19,... | collective-permute-start | bytes 41480 | tf_op jit(solution)/shard_map/ppermute | solution.py:24
  124.8 3.8 %copy-start.3 = (f32[12,36,260]{2,1,0:T(8,128)}, f32[12,36,260]{2,1,0:T(8,128)S(1)}, u32[]{:S(2)}) copy-start(f32[12,36,260]{2,1,0:T(8,128)S(1)} %get-tuple-element.33) | copy-start | bytes 1347844
  131.8 1.6 copy-start.14
  132.9 34.3 %copy-start.4 = (f32[12,36,260]{2,1,0:T(8,128)S(1)}, f32[12,36,260]{2,1,0:T(8,128)}, u32[]{:S(2)}) copy-start(f32[12,36,260]{2,1,0:T(8,128)} %copy-done.3) | copy-start | bytes 1347844
  (5 other events, 6.4 us)
